TPU v7x, 32 devices: a whole 2x2x4 slice. The times are simulated.
32 devices in a mesh: cell: 16 (over z, y, x), gene: 2 (over core).
Axes of the slice: x: 2, y: 2, z: 4, core: 2. Of those that a mesh axis runs over, the one named last changes fastest.
Arguments:
- tiles: bfloat16 [2, 1024, 128, 128], P('gene', 'cell'), may hold values from -8 to 8
- tile_row: int32 [2, 1024], P('gene', 'cell'), may hold values from 0 to 7, as said below
- tile_col: int32 [2, 1024], P('gene', 'cell'), may hold values from 0 to 15
- tile_count: int32 [2, 16], P('gene', 'cell'), may hold values from 1 to 64, as said below
- start_basis: bfloat16 [64, 4096], P(None, 'gene'), may hold values from -0.09375 to 0.09375
Outputs:
- basis: bfloat16 [64, 16384], P(None, 'cell')
- loadings: float32 [64, 4096], P(None, ('gene', 'cell'))
Inputs may be any that keep to these rules, and one draw needn't show every extreme that they name: `tile_row`: tile row of each slot, within 0 to 7; the slots of one device name distinct (row, column) pairs. `tile_count`: slots in use; for each index of gene some device uses all 64.
All inputs are finite; a program needn't handle non-finite values.
Results may differ from a plain program's by a relative error of at most 0.018.
Values may be sent and summed in bfloat16 or wider, within the bound.
No kernel may reach another device: no remote copies, remote signals or barrier semaphores. Data moves between devices by JAX's collectives and lax.ppermute only.
A program may use at most 64 MiB of HBM per device.

v0:
```python
import jax
import jax.numpy as jnp
from jax import lax
from jax.sharding import PartitionSpec as P

ROW_BLOCKS = 8


def solve_lower(lower, right):
    return lax.linalg.triangular_solve(lower, right, left_side=True, lower=True)


def gram_of(scores):
    return jnp.dot(
        scores, scores.T, precision=lax.Precision.HIGHEST, preferred_element_type=jnp.float32
    )


def orthonormal(scores, first_total):
    first = first_total(gram_of(scores))
    lower_one = jnp.linalg.cholesky(first)
    return solve_lower(lower_one, scores)


def local(tiles, tile_row, tile_col, tile_count, start_basis):
    blocks_local = tiles[0]
    slot_count = blocks_local.shape[0]
    tile_size = blocks_local.shape[-1]
    width = start_basis.shape[0]
    gene_dev = start_basis.shape[1]
    gene_blocks = gene_dev // tile_size
    row_blocks = ROW_BLOCKS
    cell_dev = row_blocks * tile_size
    row_index = tile_row[0]
    col_index = tile_col[0]
    live = jnp.arange(slot_count) < tile_count[0, 0]
    row_target = jnp.where(live, row_index, row_blocks)
    col_target = jnp.where(live, col_index, gene_blocks)

    def first_total(gram):
        return lax.psum(gram, ("cell", "gene"))

    def merge_halves(partial_scores):
        return lax.psum_scatter(partial_scores, "gene", scatter_dimension=1, tiled=True)

    def scores_of(basis):
        picked = jnp.take(basis.reshape(width, gene_blocks, tile_size), col_index, axis=1)
        products = jnp.einsum(
            "ksg,srg->skr", picked, blocks_local, preferred_element_type=jnp.float32
        )
        summed = jax.ops.segment_sum(products, row_target, num_segments=row_blocks + 1)[:row_blocks]
        return merge_halves(jnp.transpose(summed, (1, 0, 2)).reshape(width, cell_dev))

    def loadings_of(ortho_half):
        picked = jnp.take(ortho_half.reshape(width, row_blocks, tile_size), row_index, axis=1)
        products = jnp.einsum(
            "ksr,srg->skg", picked, blocks_local, preferred_element_type=jnp.float32
        )
        summed = jax.ops.segment_sum(products, col_target, num_segments=gene_blocks + 1)[
            :gene_blocks
        ]
        return jnp.transpose(summed, (1, 0, 2)).reshape(width, gene_dev)

    ortho = orthonormal(scores_of(start_basis), first_total)
    ortho_half = ortho.astype(jnp.bfloat16)
    ortho_rows = lax.all_gather(ortho_half, "gene", axis=1, tiled=True)
    partial_value = loadings_of(ortho_rows)
    next_basis = lax.psum(partial_value, "cell").astype(jnp.bfloat16)
    ortho_two = orthonormal(scores_of(next_basis), first_total)
    scale = jnp.sqrt(jnp.float32(lax.axis_size("cell") * cell_dev))
    ortho_two_half = ortho_two.astype(jnp.bfloat16)
    basis_piece = (ortho_two * scale).astype(jnp.bfloat16)
    final_rows, basis = (
        lax.all_gather(ortho_two_half, "gene", axis=1, tiled=True),
        lax.all_gather(basis_piece, "gene", axis=1, tiled=True),
    )
    loadings = lax.psum_scatter(loadings_of(final_rows), "cell", scatter_dimension=1, tiled=True)
    return (basis, loadings)


def solution(mesh):
    return jax.shard_map(
        local,
        mesh=mesh,
        in_specs=(
            P("gene", "cell", None, None),
            P("gene", "cell"),
            P("gene", "cell"),
            P("gene", "cell"),
            P(None, "gene"),
        ),
        out_specs=(P(None, "cell"), P(None, ("gene", "cell"))),
        check_vma=False,
    )
```

profile of v0, /device:TPU:0, one launch (start us, length us, event | category | flops | bytes accessed | tf_op | source)
XLA Modules:
  0.0 349.9 jit_solution(15291023441210544630)
XLA Ops:
  11.2 2.9 fusion.6
  14.1 7.1 %scatter_fusion = f32[9,64,128]{2,1,0:T(8,128)S(1)} fusion(f32[9,64,128]{2,1,0:T(8,128)S(1)} %broadcast.69.clone, s32[64]{0:T(128)S(1)} %get-tuple-element.8, f32[64,64,128]{2,1,0:T(8,128)} %fusion.6), kind=kCustom, calls=%fused_computation.4 | custom fusion | flops 524288 | bytes 6291712 | tf_op jit(solution)/shard_map/scatter-add | solution.py:51
  22.0 10.5 %reduce-scatter.4.cloned.1.call-done = f32[64,512]{1,0:T(8,128)} async-done(((f32[64,1024]{1,0:T(8,128)}), f32[64,512]{1,0:T(8,128)}) %reduce-scatter.4.cloned.1.call-update) | async-done | bytes 131088 | tf_op jit(solution)/shard_map/reduce_scatter | solution.py:44
  32.5 1.2 fusion.40
  33.8 40.5 %psum.21 = f32[64,64]{0,1:T(8,128)S(1)} all-reduce(f32[64,64]{0,1:T(8,128)S(1)} %fusion.40), channel_id=1, replica_groups=mesh['cell'=16,'gene'=2] {'cell','gene'}, use_global_device_ids=true, to_apply=%region_2.4 | all-reduce | flops 4096 | bytes 32768 | tf_op jit(solution)/shard_map/psum | solution.py:41
  74.4 5.8 %cholesky.44 = f32[64,64]{1,0:T(8,128)S(1)} custom-call(f32[64,64]{1,0:T(8,128)S(1)} %fusion.30), custom_call_target="Cholesky" | custom-call | tf_op jit(solution)/shard_map/jit(cholesky)/cholesky | solution.py:21
  81.6 4.9 %custom-call.6 = f32[1,64,64]{1,2,0:T(8,128)S(1)} custom-call(f32[1,64,64]{2,1,0:T(8,128)S(1)} %fusion.24), custom_call_target="InvertDiagBlocksLowerTriangular" | custom-call | tf_op jit(solution)/shard_map/triangular_solve/custom-call.0 | solution.py:10
  86.5 1.2 convolution_convert_fusion
  87.7 1.9 all_gather.9
  90.4 2.1 fusion.4
  92.6 7.1 %scatter_fusion.1 = f32[17,64,128]{2,1,0:T(8,128)S(1)} fusion(f32[17,64,128]{2,1,0:T(8,128)S(1)} %broadcast.70.clone, s32[64]{0:T(128)S(1)} %get-tuple-element.9, f32[64,64,128]{2,1,0:T(8,128)} %fusion.4), kind=kCustom, calls=%fused_computation.5 | custom fusion | flops 524288 | bytes 6291712 | tf_op jit(solution)/shard_map/scatter-add | solution.py:59
  99.7 81.7 %all-reduce.1 = bf16[64,2048]{1,0:T(8,128)(2,1)S(1)} all-reduce(f32[64,2048]{1,0:T(8,128)S(1)} %copy_bitcast_fusion.1), channel_id=1, replica_groups=mesh['cell'=16,'gene'=2] {'cell'}, use_global_device_ids=true, to_apply=%region_6.11 | all-reduce | flops 131072 | bytes 786432 | tf_op jit(solution)/shard_map/psum | solution.py:68
  182.2 2.9 fusion.2
  185.1 7.1 %scatter_fusion.2 = f32[9,64,128]{2,1,0:T(8,128)S(1)} fusion(f32[9,64,128]{2,1,0:T(8,128)S(1)} %broadcast.69, s32[64]{0:T(128)S(1)} %get-tuple-element.8, f32[64,64,128]{2,1,0:T(8,128)} %fusion.2), kind=kCustom, calls=%fused_computation.6 | custom fusion | flops 524288 | bytes 6291712 | tf_op jit(solution)/shard_map/scatter-add | solution.py:51
  192.9 4.2 %reduce-scatter.6.cloned.1.call-done = f32[64,512]{1,0:T(8,128)} async-done(((f32[64,1024]{1,0:T(8,128)}), f32[64,512]{1,0:T(8,128)}) %reduce-scatter.6.cloned.1.call-update) | async-done | bytes 131088 | tf_op jit(solution)/shard_map/reduce_scatter | solution.py:44
  198.4 40.8 %psum.23 = f32[64,64]{0,1:T(8,128)S(1)} all-reduce(f32[64,64]{0,1:T(8,128)S(1)} %fusion.41), channel_id=1, replica_groups=mesh['cell'=16,'gene'=2] {'cell','gene'}, use_global_device_ids=true, to_apply=%region_9.14 | all-reduce | flops 4096 | bytes 32768 | tf_op jit(solution)/shard_map/psum | solution.py:41
  239.2 5.8 %cholesky.55 = f32[64,64]{1,0:T(8,128)S(1)} custom-call(f32[64,64]{1,0:T(8,128)S(1)} %fusion.28), custom_call_target="Cholesky" | custom-call | tf_op jit(solution)/shard_map/jit(cholesky)/cholesky | solution.py:21
  246.4 4.9 %custom-call.7 = f32[1,64,64]{1,2,0:T(8,128)S(1)} custom-call(f32[1,64,64]{2,1,0:T(8,128)S(1)} %fusion.25), custom_call_target="InvertDiagBlocksLowerTriangular" | custom-call | tf_op jit(solution)/shard_map/triangular_solve/custom-call.0 | solution.py:10
  251.3 1.2 fusion.39
  252.6 1.9 all_gather.11
  255.2 2.1 fusion
  257.4 7.1 %scatter_fusion.3 = f32[17,64,128]{2,1,0:T(8,128)S(1)} fusion(f32[17,64,128]{2,1,0:T(8,128)S(1)} %broadcast.70, s32[64]{0:T(128)S(1)} %get-tuple-element.9, f32[64,64,128]{2,1,0:T(8,128)} %fusion), kind=kCustom, calls=%fused_computation.7 | custom fusion | flops 524288 | bytes 6291712 | tf_op jit(solution)/shard_map/scatter-add | solution.py:59
  265.3 1.9 all_gather.10
  267.2 75.5 %reduce-scatter.8.cloned.1.call-done = f32[64,128]{1,0:T(8,128)} async-done(((f32[64,2048]{1,0:T(8,128)}), f32[64,128]{1,0:T(8,128)}) %reduce-scatter.8.cloned.1.call-update) | async-done | bytes 32784 | tf_op jit(solution)/shard_map/reduce_scatter | solution.py:77
  (47 shorter events, 12.9 us)
Async XLA Ops:
  7.2 4.0 %copy-start = (bf16[1,64,128,128]{3,2,1,0:T(8,128)(2,1)S(1)}, bf16[1,64,128,128]{3,2,1,0:T(8,128)(2,1)}, u32[]{:S(2)}) copy-start(bf16[1,64,128,128]{3,2,1,0:T(8,128)(2,1)} %param.12) | copy-start | bytes 6291460
  7.2 4.0 %copy-start.1 = (s32[1,64]{1,0:T(1,128)S(1)}, s32[1,64]{1,0:T(1,128)}, u32[]{:S(2)}) copy-start(s32[1,64]{1,0:T(1,128)} %param.14) | copy-start | bytes 772
  7.2 4.0 %copy-start.2 = (s32[1,64]{1,0:T(1,128)S(1)}, s32[1,64]{1,0:T(1,128)}, u32[]{:S(2)}) copy-start(s32[1,64]{1,0:T(1,128)} %param.13) | copy-start | bytes 772
  7.2 25.3 %reduce-scatter.4.cloned.1.call-start = ((), (), s32[]{:S(2)}) async-start(), calls=%async_computation.3 | async-start | bytes 393216 | tf_op jit(solution)/shard_map/reduce_scatter | solution.py:44
  21.9 175.2 %reduce-scatter.6.cloned.1.call-start = ((), (), s32[]{:S(2)}) async-start(), calls=%async_computation.4 | async-start | bytes 393216 | tf_op jit(solution)/shard_map/reduce_scatter | solution.py:44
  192.9 149.8 %reduce-scatter.8.cloned.1.call-start = ((), (), s32[]{:S(2)}) async-start(), calls=%async_computation.5 | async-start | bytes 557056 | tf_op jit(solution)/shard_map/reduce_scatter | solution.py:77
Sparse Core Ops, SparseCore 0:
  22.0 10.4 reduce-scatter.3
  193.0 4.0 reduce-scatter.5
  265.4 77.2 reduce-scatter.7
where the time goes:
time: 351 us; the launch traced here: 350 us
  blocking collectives  169 us (48%)
  waiting for transfers between devices  90.3 us (26%)
  other arithmetic  53.9 us (15%)
  matrix products  14.9 us (4%)
  between operations  14.7 us (4%)
  local copies, waits for them, and re-layouts  7.35 us (2%)
    psum x1, blocking collectives, local(): next_basis = lax.psum(partial_value, 'cell').astype(jnp.bfloat16)  81.7 us
    psum x2, blocking collectives, first_total(): return lax.psum(gram, ('cell', 'gene'))  81.3 us
    reduce_scatter x1, waiting for transfers between devices, local(): lax.psum_scatter(loadings_of(final_rows), 'cell', scatter_dimension=1, ti...  75.5 us
    reduce_scatter x2, waiting for transfers between devices, merge_halves(): lax.psum_scatter(partial_scores, 'gene', scatter_dimension=1, tiled=True)  14.7 us
    scatter-add x2, other arithmetic, scores_of(): jax.ops.segment_sum(products, row_target, num_segments=row_blocks + 1)  14.1 us
    scatter-add x2, other arithmetic, loadings_of(): jax.ops.segment_sum(products, col_target, num_segments=gene_blocks + 1)  14.1 us
    another operation x6, other arithmetic, orthonormal(): lower_one = jnp.linalg.cholesky(first)  13 us
    another operation x4, other arithmetic, solve_lower(): return lax.linalg.triangular_solve(lower, right, left_side=True, lower=True)  11.1 us
  transfers between devices with their start and end apart: 3, of which 3 were waited for; matrix products, arithmetic and copies ran while one was open for 0% of the time, Pallas kernels for 0%

commit v1 on v0

--- a/solution.py
+++ b/solution.py
@@ -38,7 +38,7 @@
     col_target = jnp.where(live, col_index, gene_blocks)
 
     def first_total(gram):
-        return lax.psum(gram, ("cell", "gene"))
+        return jax.lax.psum(jax.lax.psum(gram, "gene"), "cell")
 
     def merge_halves(partial_scores):
         return lax.psum_scatter(partial_scores, "gene", scatter_dimension=1, tiled=True)

time: 351 us -> 425 us (1.21)
  blocking collectives: 169 us -> 244 us
    psum x2 -> x4, blocking collectives: 81.3 us -> 161 us  [first_total(): return jax.lax.psum(jax.lax.psum(gram, 'gene'), 'cell')]
    psum x1, blocking collectives: 81.7 us -> 77.3 us  [local(): next_basis = lax.psum(partial_value, 'cell').astype(jnp.bfloat16)]
where the time goes in v1:
time: 425 us; the launch traced here: 423 us
  blocking collectives  244 us (57%)
  waiting for transfers between devices  88.4 us (21%)
  other arithmetic  53.9 us (13%)
  matrix products  14.9 us (4%)
  between operations  14.7 us (3%)
  local copies, waits for them, and re-layouts  7.35 us (2%)
    psum x4, blocking collectives, first_total(): return jax.lax.psum(jax.lax.psum(gram, 'gene'), 'cell')  161 us
    psum x1, blocking collectives, local(): next_basis = lax.psum(partial_value, 'cell').astype(jnp.bfloat16)  77.3 us
    reduce_scatter x1, waiting for transfers between devices, local(): lax.psum_scatter(loadings_of(final_rows), 'cell', scatter_dimension=1, ti...  71.8 us
    reduce_scatter x2, waiting for transfers between devices, merge_halves(): lax.psum_scatter(partial_scores, 'gene', scatter_dimension=1, tiled=True)  16.6 us
    scatter-add x2, other arithmetic, scores_of(): jax.ops.segment_sum(products, row_target, num_segments=row_blocks + 1)  14.1 us
    scatter-add x2, other arithmetic, loadings_of(): jax.ops.segment_sum(products, col_target, num_segments=gene_blocks + 1)  14.1 us
    another operation x6, other arithmetic, orthonormal(): lower_one = jnp.linalg.cholesky(first)  13 us
    another operation x4, other arithmetic, solve_lower(): return lax.linalg.triangular_solve(lower, right, left_side=True, lower=True)  11.1 us
  transfers between devices with their start and end apart: 3, of which 3 were waited for; matrix products, arithmetic and copies ran while one was open for 0% of the time, Pallas kernels for 0%

profile of v1, /device:TPU:0, one launch (start us, length us, event | category | flops | bytes accessed | tf_op | source)
XLA Modules:
  0.0 423.5 jit_solution(1674512681813735329)
XLA Ops:
  11.2 2.9 fusion.6
  14.1 7.1 %scatter_fusion = f32[9,64,128]{2,1,0:T(8,128)S(1)} fusion(f32[9,64,128]{2,1,0:T(8,128)S(1)} %broadcast.69.clone, s32[64]{0:T(128)S(1)} %get-tuple-element.8, f32[64,64,128]{2,1,0:T(8,128)} %fusion.6), kind=kCustom, calls=%fused_computation.4 | custom fusion | flops 524288 | bytes 6291712 | tf_op jit(solution)/shard_map/scatter-add | solution.py:51
  22.0 10.5 %reduce-scatter.4.cloned.1.call-done = f32[64,512]{1,0:T(8,128)} async-done(((f32[64,1024]{1,0:T(8,128)}), f32[64,512]{1,0:T(8,128)}) %reduce-scatter.4.cloned.1.call-update) | async-done | bytes 131088 | tf_op jit(solution)/shard_map/reduce_scatter | solution.py:44
  33.8 3.4 psum.35
  37.2 77.1 %psum.36 = f32[64,64]{0,1:T(8,128)S(1)} all-reduce(f32[64,64]{0,1:T(8,128)S(1)} %psum.35), channel_id=1, replica_groups=mesh['cell'=16,'gene'=2] {'cell'}, use_global_device_ids=true, to_apply=%region_3.5 | all-reduce | flops 4096 | bytes 32768 | tf_op jit(solution)/shard_map/psum | solution.py:41
  114.4 5.8 %cholesky.44 = f32[64,64]{1,0:T(8,128)S(1)} custom-call(f32[64,64]{1,0:T(8,128)S(1)} %fusion.30), custom_call_target="Cholesky" | custom-call | tf_op jit(solution)/shard_map/jit(cholesky)/cholesky | solution.py:21
  121.6 4.9 %custom-call.6 = f32[1,64,64]{1,2,0:T(8,128)S(1)} custom-call(f32[1,64,64]{2,1,0:T(8,128)S(1)} %fusion.24), custom_call_target="InvertDiagBlocksLowerTriangular" | custom-call | tf_op jit(solution)/shard_map/triangular_solve/custom-call.0 | solution.py:10
  127.7 1.9 all_gather.9
  130.4 2.1 fusion.4
  132.6 7.1 %scatter_fusion.1 = f32[17,64,128]{2,1,0:T(8,128)S(1)} fusion(f32[17,64,128]{2,1,0:T(8,128)S(1)} %broadcast.70.clone, s32[64]{0:T(128)S(1)} %get-tuple-element.9, f32[64,64,128]{2,1,0:T(8,128)} %fusion.4), kind=kCustom, calls=%fused_computation.5 | custom fusion | flops 524288 | bytes 6291712 | tf_op jit(solution)/shard_map/scatter-add | solution.py:59
  139.7 77.3 %all-reduce.1 = bf16[64,2048]{1,0:T(8,128)(2,1)S(1)} all-reduce(f32[64,2048]{1,0:T(8,128)S(1)} %copy_bitcast_fusion.1), channel_id=1, replica_groups=mesh['cell'=16,'gene'=2] {'cell'}, use_global_device_ids=true, to_apply=%region_7.12 | all-reduce | flops 131072 | bytes 786432 | tf_op jit(solution)/shard_map/psum | solution.py:68
  217.8 2.9 fusion.2
  220.7 7.1 %scatter_fusion.2 = f32[9,64,128]{2,1,0:T(8,128)S(1)} fusion(f32[9,64,128]{2,1,0:T(8,128)S(1)} %broadcast.69, s32[64]{0:T(128)S(1)} %get-tuple-element.8, f32[64,64,128]{2,1,0:T(8,128)} %fusion.2), kind=kCustom, calls=%fused_computation.6 | custom fusion | flops 524288 | bytes 6291712 | tf_op jit(solution)/shard_map/scatter-add | solution.py:51
  228.5 6.1 %reduce-scatter.6.cloned.1.call-done = f32[64,512]{1,0:T(8,128)} async-done(((f32[64,1024]{1,0:T(8,128)}), f32[64,512]{1,0:T(8,128)}) %reduce-scatter.6.cloned.1.call-update) | async-done | bytes 131088 | tf_op jit(solution)/shard_map/reduce_scatter | solution.py:44
  235.9 3.4 psum.38
  239.3 77.1 %psum.39 = f32[64,64]{0,1:T(8,128)S(1)} all-reduce(f32[64,64]{0,1:T(8,128)S(1)} %psum.38), channel_id=1, replica_groups=mesh['cell'=16,'gene'=2] {'cell'}, use_global_device_ids=true, to_apply=%region_11.16 | all-reduce | flops 4096 | bytes 32768 | tf_op jit(solution)/shard_map/psum | solution.py:41
  316.6 5.8 %cholesky.55 = f32[64,64]{1,0:T(8,128)S(1)} custom-call(f32[64,64]{1,0:T(8,128)S(1)} %fusion.28), custom_call_target="Cholesky" | custom-call | tf_op jit(solution)/shard_map/jit(cholesky)/cholesky | solution.py:21
  323.7 4.9 %custom-call.7 = f32[1,64,64]{1,2,0:T(8,128)S(1)} custom-call(f32[1,64,64]{2,1,0:T(8,128)S(1)} %fusion.25), custom_call_target="InvertDiagBlocksLowerTriangular" | custom-call | tf_op jit(solution)/shard_map/triangular_solve/custom-call.0 | solution.py:10
  328.6 1.2 fusion.39
  329.9 1.9 all_gather.11
  332.6 2.1 fusion
  334.7 7.1 %scatter_fusion.3 = f32[17,64,128]{2,1,0:T(8,128)S(1)} fusion(f32[17,64,128]{2,1,0:T(8,128)S(1)} %broadcast.70, s32[64]{0:T(128)S(1)} %get-tuple-element.9, f32[64,64,128]{2,1,0:T(8,128)} %fusion), kind=kCustom, calls=%fused_computation.7 | custom fusion | flops 524288 | bytes 6291712 | tf_op jit(solution)/shard_map/scatter-add | solution.py:59
  342.6 1.9 all_gather.10
  344.5 71.8 %reduce-scatter.8.cloned.1.call-done = f32[64,128]{1,0:T(8,128)} async-done(((f32[64,2048]{1,0:T(8,128)}), f32[64,128]{1,0:T(8,128)}) %reduce-scatter.8.cloned.1.call-update) | async-done | bytes 32784 | tf_op jit(solution)/shard_map/reduce_scatter | solution.py:77
  (49 shorter events, 15.4 us)
Async XLA Ops:
  7.2 4.0 copy-start
  7.2 4.0 copy-start.1
  7.2 4.0 copy-start.2
  7.2 25.3 %reduce-scatter.4.cloned.1.call-start = ((), (), s32[]{:S(2)}) async-start(), calls=%async_computation.3 | async-start | bytes 393216 | tf_op jit(solution)/shard_map/reduce_scatter | solution.py:44
  21.9 212.8 %reduce-scatter.6.cloned.1.call-start = ((), (), s32[]{:S(2)}) async-start(), calls=%async_computation.4 | async-start | bytes 393216 | tf_op jit(solution)/shard_map/reduce_scatter | solution.py:44
  228.5 187.8 %reduce-scatter.8.cloned.1.call-start = ((), (), s32[]{:S(2)}) async-start(), calls=%async_computation.5 | async-start | bytes 557056 | tf_op jit(solution)/shard_map/reduce_scatter | solution.py:77
Sparse Core Ops, SparseCore 0:
  22.0 10.4 reduce-scatter.3
  228.6 5.9 reduce-scatter.5
  342.7 73.4 reduce-scatter.7
